TPU v7x, 32 devices: a whole 2x2x4 slice. The times are simulated.
32 devices in a mesh: groups: 2 (over x), expert: 16 (over z, y, core).
Axes of the slice: x: 2, y: 2, z: 4, core: 2. Of those that a mesh axis runs over, the one named last changes fastest.
Arguments:
- tokens: bfloat16 [1024, 2048], P(('groups', 'expert')), parts along dimension 0, may hold values from -6 to 6
- expert_ids: int32 [1024, 2], P(('groups', 'expert')), parts along dimension 0, may hold values from 0 to 7, all different within a row; in each aligned block of 32 rows (0 to 31, 32 to 63, ...) at most 16 rows name the same one
- member_ids: int32 [1024], P(('groups', 'expert')), parts along dimension 0, may hold values from 0 to 7
- combine_weights: float32 [1024, 2], P(('groups', 'expert')), parts along dimension 0, may hold values from 0.25 to 1
- gate_weight: bfloat16 [2048, 57344], P(None, 'expert'), may hold values from -0.125 to 0.125
- up_weight: bfloat16 [2048, 57344], P(None, 'expert'), may hold values from -0.125 to 0.125
- down_weight: bfloat16 [57344, 2048], P('expert'), may hold values from -0.0625 to 0.0625
- input_factors: float32 [8, 8, 4096], replicated, may hold values from 0.5 to 2
- hidden_factors: float32 [8, 2, 57344], P(None, None, 'expert'), may hold values from 0.5 to 2
- output_factors: float32 [8, 8, 2048], replicated, may hold values from 0.5 to 2
Outputs:
- mixed: bfloat16 [1024, 2048], P(('groups', 'expert')), parts along dimension 0
There are 2 independent parts, one for each index of `groups`. A program takes and returns all parts, laid end to end along the dimension named above; an argument that names none is the same for every part. Nothing has to cross between parts.
Inputs may be any that keep to these rules, and one draw needn't show every extreme that they name: `expert_ids`: the two experts of a token differ. Among the 32 tokens of one device no expert is named more than 16 times.
All inputs are finite; a program needn't handle non-finite values.
Results may differ from a plain program's by a relative error of at most 0.012.
Values may be sent and summed in bfloat16 or wider, within the bound.
A program may use at most 128 MiB of HBM per device.

v0:
```python
import functools

import jax
import jax.numpy as jnp
from jax import lax
from jax.experimental import pallas as pl
from jax.experimental.pallas import tpu as pltpu
from jax.sharding import PartitionSpec as P

EXPERTS = 8
CAP = 16
LANES = 128
CHUNKS = 4
BATCHES = ((0, 1, 4, 6), (2, 3, 5, 7))
PLACE = {k: (b, i) for b, ks in enumerate(BATCHES) for i, k in enumerate(ks)}
BF16 = jnp.bfloat16
F32 = jnp.float32


def tile_of(size):
    for tile in (512, 256, 128):
        if size % tile == 0:
            return tile
    return size


def parts_of(table):
    high = table.astype(BF16).astype(F32)
    rest = table - high
    mid = rest.astype(BF16).astype(F32)
    low = (rest - mid).astype(BF16).astype(F32)
    return high, mid, low


def kernel(
    n,
    ids_ref,
    mem_ref,
    cw_ref,
    tok_hbm,
    hidf_hbm,
    wg_hbm,
    wu_hbm,
    wd_hbm,
    inf_hbm,
    outf_hbm,
    o_ref,
    tok_ref,
    hidf_ref,
    wg,
    wu,
    wd,
    inf,
    outf,
    tab_in,
    tab_hid,
    tab_out,
    send,
    recv,
    gate_in,
    up_in,
    hidden,
    psend,
    precv,
    osend,
    home,
    placing,
    wsem,
    fsem,
    dsend,
    drecv,
    psems,
    precs,
    hsend,
    hrecv,
    xsend,
    xrecv,
):
    split = n // EXPERTS
    toks, width = tok_ref.shape
    units = wg.shape[1]
    members = inf.shape[0]
    seg = EXPERTS * CAP
    me = lax.axis_index("expert")
    own = lax.div(me, split)
    part = lax.rem(me, split)

    def expert_at(k):
        return lax.bitwise_xor(own, k)

    def part_at(j):
        return lax.rem(part + (j + split) % split, split)

    def far(k):
        return {"expert": expert_at(k) * split + part}

    def near(j):
        return {"expert": own * split + part_at(j)}

    def rows(index, count=CAP):
        return pl.ds(pl.multiple_of(index * count, count), count)

    barrier = pltpu.get_barrier_semaphore()
    for k in range(1, EXPERTS):
        pl.semaphore_signal(barrier, inc=1, device_id=far(k), device_id_type=pl.DeviceIdType.MESH)
    for j in range(1, split):
        pl.semaphore_signal(barrier, inc=1, device_id=near(j), device_id_type=pl.DeviceIdType.MESH)

    loads = [
        pltpu.make_async_copy(inf_hbm.at[own], inf, fsem.at[0]),
        pltpu.make_async_copy(hidf_hbm, hidf_ref, fsem.at[2]),
        pltpu.make_async_copy(outf_hbm.at[own], outf, fsem.at[1]),
    ]
    weights = []
    for index, (src, dst) in enumerate(((wg_hbm, wg), (wu_hbm, wu), (wd_hbm, wd))):
        step = src.shape[0] // CHUNKS
        weights.append(
            [
                pltpu.make_async_copy(
                    src.at[pl.ds(c * step, step)], dst.at[pl.ds(c * step, step)], wsem.at[index, c]
                )
                for c in range(CHUNKS)
            ]
        )
    tok_load = pltpu.make_async_copy(tok_hbm, tok_ref, fsem.at[3])
    for copy in [tok_load] + loads + weights[0] + weights[1]:
        copy.start()

    down_i = lax.broadcasted_iota(jnp.int32, (toks, toks), 0)
    across = lax.broadcasted_iota(jnp.int32, (toks, toks), 1)

    def column(row):
        spread = jnp.broadcast_to(row.astype(F32), (toks, toks))
        return jnp.sum(jnp.where(across == down_i, spread, 0.0), axis=1, keepdims=True)

    lane = lax.broadcasted_iota(jnp.int32, (toks, seg), 1)
    lane_expert = lax.shift_right_logical(lane, CAP.bit_length() - 1)
    lane_slot = lax.bitwise_and(lane, CAP - 1)
    hit0 = column(ids_ref[0:1, :]) == lane_expert.astype(F32)
    hit1 = column(ids_ref[1:2, :]) == lane_expert.astype(F32)
    named = jnp.where(hit0 | hit1, 1.0, 0.0)
    earlier = jnp.where(across < down_i, 1.0, 0.0)
    rank = jnp.dot(earlier.astype(BF16), named.astype(BF16), preferred_element_type=F32)
    placed = jnp.where(rank == lane_slot.astype(F32), named, 0.0)
    placing[...] = placed.astype(BF16)
    member = column(mem_ref[...])
    col = lax.broadcasted_iota(jnp.int32, (toks, LANES), 1)
    col_member = lax.rem(col, members).astype(F32)
    onehot = jnp.where((col < 3 * members) & (col_member == member), 1.0, 0.0)

    def gather(which, data):
        return lax.dot_general(
            which.astype(BF16), data.astype(BF16), (((0,), (0,)), ((), ())), preferred_element_type=F32
        )

    meta_rows = jnp.zeros((seg, LANES), F32)
    for route, hit in ((0, hit0), (1, hit1)):
        meta = onehot
        for spot, piece in enumerate(parts_of(column(cw_ref[route : route + 1, :]))):
            meta = jnp.where(col == 3 * members + spot, piece, meta)
        meta_rows = meta_rows + gather(jnp.where(hit, placed, 0.0), meta)
    send[:, width:] = meta_rows.astype(BF16)
    wide = tile_of(width)
    tok_load.wait()
    for t in range(width // wide):
        cols = slice(t * wide, (t + 1) * wide)
        send[:, cols] = gather(placed, tok_ref[:, cols]).astype(BF16)

    pl.semaphore_wait(barrier, EXPERTS - 1 + split - 1)

    def direct(k):
        return pltpu.make_async_remote_copy(
            src_ref=send.at[rows(expert_at(k))],
            dst_ref=recv.at[landed(k, 0)],
            send_sem=dsend.at[k],
            recv_sem=drecv.at[k],
            device_id=far(k),
            device_id_type=pl.DeviceIdType.MESH,
        )

    def landed(k, j):
        batch, slot = PLACE[k]
        each = len(BATCHES[batch])
        return rows(batch * split * each + part_at(-j) * each + slot)

    def handed(k, j):
        return pltpu.make_async_remote_copy(
            src_ref=recv.at[landed(k, 0)] if k else send.at[rows(own)],
            dst_ref=recv.at[landed(k, 0)],
            send_sem=xsend.at[k, j],
            recv_sem=xrecv.at[k, j],
            device_id=near(j),
            device_id_type=pl.DeviceIdType.MESH,
        )

    for k in BATCHES[0] + BATCHES[1]:
        if k:
            direct(k).start()
    for j in range(1, split):
        handed(0, j).start()
    recv[landed(0, 0), :] = send[rows(own), :]

    for copy in loads:
        copy.wait()
    for tab in (tab_in, tab_hid, tab_out):
        tab[...] = jnp.zeros(tab.shape, tab.dtype)

    def fill(tab, at, table):
        high, mid, low = parts_of(table)
        pad = jnp.zeros_like(high)
        tab[0 : 4 * members, at : at + table.shape[1]] = jnp.concatenate(
            [high, mid, low, pad], axis=0
        ).astype(BF16)

    for t in range(2 * width // wide):
        fill(tab_in, t * wide, inf[:, t * wide : (t + 1) * wide])
    for t in range(width // wide):
        fill(tab_out, t * wide, outf[:, t * wide : (t + 1) * wide])
    tile = tile_of(units)
    for g in range(2):
        for t in range(units // tile):
            fill(tab_hid, g * units + t * tile, hidf_ref[:, g, t * tile : (t + 1) * tile])

    for copy in weights[2]:
        copy.start()

    def hand_on(ks):
        for k in ks:
            if k:
                pltpu.make_async_remote_copy(
                    src_ref=recv.at[landed(k, 0)],
                    dst_ref=recv.at[landed(k, 0)],
                    send_sem=dsend.at[k],
                    recv_sem=drecv.at[k],
                    device_id=far(k),
                    device_id_type=pl.DeviceIdType.MESH,
                ).wait_recv()
                for j in range(1, split):
                    handed(k, j).start()

    tiles, _, out_tile = home.shape
    batch_rows = recv.shape[0] // len(BATCHES)
    share_rows = batch_rows // split

    def scale_inputs(b):
        for k in BATCHES[b]:
            for j in range(1, split):
                pltpu.make_async_remote_copy(
                    src_ref=recv.at[landed(k, j)],
                    dst_ref=recv.at[landed(k, j)],
                    send_sem=xsend.at[k, j],
                    recv_sem=xrecv.at[k, j],
                    device_id=near(j),
                    device_id_type=pl.DeviceIdType.MESH,
                ).wait_recv()
        mine = slice(b * batch_rows, (b + 1) * batch_rows)
        meta = recv[mine, width:]
        for t in range(width // wide):
            cols = slice(t * wide, (t + 1) * wide)
            data = recv[mine, cols].astype(F32)
            scale = jnp.dot(meta, tab_in[:, cols], preferred_element_type=F32)
            gate_in[:, cols] = (data * scale).astype(BF16)
            cols_up = slice(width + t * wide, width + (t + 1) * wide)
            scale = jnp.dot(meta, tab_in[:, cols_up], preferred_element_type=F32)
            up_in[:, cols] = (data * scale).astype(BF16)

    def hidden_units(b):
        mine = slice(b * batch_rows, (b + 1) * batch_rows)

        def hidden_tile(t, carry):
            cols = pl.ds(pl.multiple_of(t * tile, tile), tile)
            cols_up = pl.ds(pl.multiple_of(units + t * tile, LANES), tile)
            meta = recv[mine, width:]
            gate = jnp.dot(gate_in[...], wg[:, cols], preferred_element_type=F32)
            gate = gate * jnp.dot(meta, tab_hid[:, cols], preferred_element_type=F32)
            up = jnp.dot(up_in[...], wu[:, cols], preferred_element_type=F32)
            up = up * jnp.dot(meta, tab_hid[:, cols_up], preferred_element_type=F32)
            hidden[:, cols] = (gate / (1.0 + jnp.exp(-gate)) * up).astype(BF16)
            return carry

        lax.fori_loop(0, units // tile, hidden_tile, 0)

    def share(b, t, j):
        return pltpu.make_async_remote_copy(
            src_ref=psend.at[b, t, rows(part_at(j), share_rows)],
            dst_ref=precv.at[b, t, j],
            send_sem=psems.at[b, t, j],
            recv_sem=precs.at[b, t, j],
            device_id=near(j),
            device_id_type=pl.DeviceIdType.MESH,
        )

    def back(t, k):
        batch, slot = PLACE[k]
        return pltpu.make_async_remote_copy(
            src_ref=osend.at[batch, t, pl.ds(slot * CAP, CAP)],
            dst_ref=home.at[t, rows(own)],
            send_sem=hsend.at[t, k],
            recv_sem=hrecv.at[t, k],
            device_id=far(k),
            device_id_type=pl.DeviceIdType.MESH,
        )

    def down_tile(b, t):
        cols = slice(t * out_tile, (t + 1) * out_tile)
        psend[b, t] = jnp.dot(hidden[...], wd[:, cols], preferred_element_type=F32).astype(BF16)
        for j in range(1, split):
            share(b, t, j).start()

    def finish(b, t):
        first = len(BATCHES[0]) * CAP * split * b
        meta = recv[pl.ds(pl.multiple_of(first + part * share_rows, CAP), share_rows), width:]
        spot = lax.broadcasted_iota(jnp.int32, (share_rows, LANES), 1)
        weight = jnp.sum(
            jnp.where((spot >= 3 * members) & (spot < 3 * members + 3), meta.astype(F32), 0.0),
            axis=1,
            keepdims=True,
        )
        total = psend[b, t, rows(part, share_rows), :].astype(F32)
        for j in range(1, split):
            share(b, t, j).wait_recv()
            total = total + precv[b, t, j].astype(F32)
        cols = slice(t * out_tile, (t + 1) * out_tile)
        scale = jnp.dot(meta, tab_out[:, cols], preferred_element_type=F32)
        value = (total * scale * weight).astype(BF16)
        osend[b, t] = value
        for slot, k in enumerate(BATCHES[b]):
            if k:
                back(t, k).start()
            else:
                home[t, rows(own), :] = value[slot * CAP : (slot + 1) * CAP]

    hand_on(BATCHES[0])
    scale_inputs(0)
    for copy in weights[0] + weights[1]:
        copy.wait()
    hidden_units(0)
    hand_on(BATCHES[1][:2])
    for copy in weights[2]:
        copy.wait()
    for t in range(tiles):
        down_tile(0, t)
        if t > 0:
            finish(0, t - 1)
        if t == tiles // 2:
            hand_on(BATCHES[1][2:])
    scale_inputs(1)
    finish(0, tiles - 1)
    hidden_units(1)
    for t in range(tiles):
        down_tile(1, t)
        if t > 0:
            finish(1, t - 1)
    finish(1, tiles - 1)

    for t in range(tiles):
        cols = slice(t * out_tile, (t + 1) * out_tile)
        for k in range(1, EXPERTS):
            back(t, k).wait_recv()
        o_ref[:, cols] = jnp.dot(placing[...], home[t], preferred_element_type=F32).astype(BF16)

    for k in range(1, EXPERTS):
        direct(k).wait_send()
    for k in range(EXPERTS):
        for j in range(1, split):
            handed(k, j).wait_send()
    for t in range(tiles):
        for b in range(len(BATCHES)):
            for j in range(1, split):
                share(b, t, j).wait_send()
        for k in range(1, EXPERTS):
            back(t, k).wait_send()


def per_device(
    tokens,
    expert_ids,
    member_ids,
    combine_weights,
    gate_weight,
    up_weight,
    down_weight,
    input_factors,
    hidden_factors,
    output_factors,
):
    n = lax.axis_size("expert")
    split = n // EXPERTS
    toks, width = tokens.shape
    units = gate_weight.shape[1]
    members = input_factors.shape[1]
    seg = EXPERTS * CAP
    all_rows = n * CAP
    batches = len(BATCHES)
    batch_rows = all_rows // batches
    out_tile = tile_of(width)
    tiles = width // out_tile
    vmem = pl.BlockSpec(memory_space=pltpu.VMEM)
    hbm = pl.BlockSpec(memory_space=pl.ANY)
    dma = pltpu.SemaphoreType.DMA
    return pl.pallas_call(
        functools.partial(kernel, n),
        out_shape=jax.ShapeDtypeStruct((toks, width), BF16),
        in_specs=[vmem] * 3 + [hbm] * 7,
        out_specs=vmem,
        scratch_shapes=[
            pltpu.VMEM((toks, width), BF16),
            pltpu.VMEM(hidden_factors.shape, F32),
            pltpu.VMEM((width, units), BF16),
            pltpu.VMEM((width, units), BF16),
            pltpu.VMEM((units, width), BF16),
            pltpu.VMEM((members, 2 * width), F32),
            pltpu.VMEM((members, width), F32),
            pltpu.VMEM((LANES, 2 * width), BF16),
            pltpu.VMEM((LANES, 2 * units), BF16),
            pltpu.VMEM((LANES, width), BF16),
            pltpu.VMEM((seg, width + LANES), BF16),
            pltpu.VMEM((all_rows, width + LANES), BF16),
            pltpu.VMEM((batch_rows, width), BF16),
            pltpu.VMEM((batch_rows, width), BF16),
            pltpu.VMEM((batch_rows, units), BF16),
            pltpu.VMEM((batches, tiles, batch_rows, out_tile), BF16),
            pltpu.VMEM((batches, tiles, split, seg // batches, out_tile), BF16),
            pltpu.VMEM((batches, tiles, seg // batches, out_tile), BF16),
            pltpu.VMEM((tiles, seg, out_tile), BF16),
            pltpu.VMEM((toks, seg), BF16),
            dma((3, CHUNKS)),
            dma((4,)),
            dma((EXPERTS,)),
            dma((EXPERTS,)),
            dma((batches, tiles, split)),
            dma((batches, tiles, split)),
            dma((tiles, EXPERTS)),
            dma((tiles, EXPERTS)),
            dma((EXPERTS, split)),
            dma((EXPERTS, split)),
        ],
        compiler_params=pltpu.CompilerParams(
            collective_id=0, has_side_effects=True, vmem_limit_bytes=67043328
        ),
        name="moe_step",
    )(
        expert_ids.T,
        member_ids.reshape(1, toks),
        combine_weights.T,
        tokens,
        hidden_factors,
        gate_weight,
        up_weight,
        down_weight,
        input_factors,
        output_factors,
    )


def solution(mesh):
    in_specs = (
        P(("groups", "expert"), None),
        P(("groups", "expert"), None),
        P(("groups", "expert")),
        P(("groups", "expert"), None),
        P(None, "expert"),
        P(None, "expert"),
        P("expert", None),
        P(),
        P(None, None, "expert"),
        P(),
    )
    out_specs = P(("groups", "expert"), None)
    return jax.shard_map(
        per_device, mesh=mesh, in_specs=in_specs, out_specs=out_specs, check_vma=False
    )
```

profile of v0, /device:TPU:0, one launch (start us, length us, event | category | flops | bytes accessed | tf_op | source)
XLA Modules:
  0.0 48.6 jit_solution(12102055908896190179)
XLA Ops:
  0.0 47.0 %moe_step.1 = bf16[32,2048]{1,0:T(8,128)(2,1)} custom-call(s32[2,32]{1,0:T(2,128)} %bitcast.3, s32[1,32]{1,0:T(1,128)} %bitcast.5, f32[2,32]{1,0:T(2,128)} %bitcast.4, bf16[32,2048]{1,0:T(8,128)(2,1)} %tok_hbm.1, f32[8,2,3584]{2,1,0:T(2,128)} %hidf_hbm.1, bf16[2048,3584]{1,0:T(8,128)(2,1)} %wg_hbm.1, bf16[2048,3584]{1,0:T(8,128)(2,1)} %wu_hbm.1, ...), custom_call_target="tpu_custom_call" | custom-call | tf_op jit(solution)/shard_map/moe_step/pallas_call | solution.py:401
  47.0 1.6 %copy.12 = bf16[32,2048]{1,0:T(8,128)(2,1)} copy(bf16[32,2048]{1,0:T(8,128)(2,1)} %moe_step.1) | data formatting | bytes 262144
where the time goes:
time: 48.7 us; the launch traced here: 48.6 us
  Pallas kernels  47 us (97%)
  local copies, waits for them, and re-layouts  1.57 us (3%)
    pallas_call x1, Pallas kernels, per_device(): pl.pallas_call(functools.partial(kernel, n), out_shape=jax.ShapeDtypeStru...  47 us
    unnamed x1, local copies, waits for them, and re-layouts  1.57 us

commit v1 on v0

v1 whole, which is shorter than its diff:
```python
import functools

import jax
import jax.numpy as jnp
from jax import lax
from jax.experimental import pallas as pl
from jax.experimental.pallas import tpu as pltpu
from jax.sharding import PartitionSpec as P

EXPERTS = 8
CAP = 16
LANES = 128
VMEM_LIMIT = 63 * 1024 * 1024
BATCHES = ((0, 1, 4, 6), (2, 3, 5, 7))
SEND_ORDER = (4, 6, 1, 2, 3, 5, 7)
PLACE = {k: (b, i) for b, ks in enumerate(BATCHES) for i, k in enumerate(ks)}
BF16 = jnp.bfloat16
F32 = jnp.float32


def tile_of(size):
    for tile in (512, 256, 128):
        if size % tile == 0:
            return tile
    return size


def parts_of(table):
    high = table.astype(BF16).astype(F32)
    rest = table - high
    mid = rest.astype(BF16).astype(F32)
    low = (rest - mid).astype(BF16).astype(F32)
    return high, mid, low


def pick(table, members):
    reps = table.shape[1] // LANES
    rows = []
    for which in members:
        full = jnp.concatenate([which] * reps, axis=1)
        rows.append(jnp.take_along_axis(table, full, axis=0, mode="promise_in_bounds"))
    return jnp.concatenate(rows, axis=0)


def kernel(
    n,
    ids_hbm,
    mem_hbm,
    cw_hbm,
    tok_hbm,
    hidf_hbm,
    wg_hbm,
    wu_hbm,
    wd_hbm,
    inf_hbm,
    outf_hbm,
    o_ref,
    ids_ref,
    mem_ref,
    cw_ref,
    tok_ref,
    hidf_ref,
    wg,
    wu,
    wd,
    inf,
    outf,
    tab_hid,
    send,
    recv,
    who,
    weigh,
    gate_in,
    up_in,
    hidden,
    psend,
    precv,
    osend,
    home,
    placing,
    wsem,
    fsem,
    dsend,
    drecv,
    psems,
    precs,
    hsend,
    hrecv,
    xsend,
    xrecv,
):
    split = n // EXPERTS
    toks, width = tok_ref.shape
    units = wg.shape[1]
    seg = EXPERTS * CAP
    me = lax.axis_index("expert")
    own = lax.div(me, split)
    part = lax.rem(me, split)
    wide = tile_of(width)
    tile = tile_of(units)
    unit_tiles = units // tile
    tiles, _, out_tile = home.shape
    batch_rows = recv.shape[0] // len(BATCHES)
    share_rows = batch_rows // split

    def expert_at(k):
        return lax.bitwise_xor(own, k)

    def part_at(j):
        return lax.rem(part + (j + split) % split, split)

    def far(k):
        return {"expert": expert_at(k) * split + part}

    def near(j):
        return {"expert": own * split + part_at(j)}

    def rows(index, count=CAP):
        return pl.ds(pl.multiple_of(index * count, count), count)

    barrier = pltpu.get_barrier_semaphore()
    for k in range(1, EXPERTS):
        pl.semaphore_signal(barrier, inc=1, device_id=far(k), device_id_type=pl.DeviceIdType.MESH)
    for j in range(1, split):
        pl.semaphore_signal(barrier, inc=1, device_id=near(j), device_id_type=pl.DeviceIdType.MESH)

    small = [
        pltpu.make_async_copy(src, dst, fsem.at[i])
        for i, (src, dst) in enumerate(
            ((ids_hbm, ids_ref), (mem_hbm, mem_ref), (cw_hbm, cw_ref), (tok_hbm, tok_ref))
        )
    ]
    loads = [
        pltpu.make_async_copy(inf_hbm.at[own], inf, fsem.at[4]),
        pltpu.make_async_copy(hidf_hbm, hidf_ref, fsem.at[5]),
        pltpu.make_async_copy(outf_hbm.at[own], outf, fsem.at[6]),
    ]

    def column_load(src, dst, size, t, sem):
        cols = pl.ds(t * size, size)
        return pltpu.make_async_copy(src.at[:, cols], dst.at[:, cols], sem)

    first = [
        [
            column_load(wg_hbm, wg, tile, t, wsem.at[0, t]),
            column_load(wu_hbm, wu, tile, t, wsem.at[1, t]),
        ]
        for t in range(unit_tiles)
    ]
    second = [column_load(wd_hbm, wd, out_tile, t, wsem.at[2, t]) for t in range(tiles)]
    for copy in small + loads:
        copy.start()
    for copy in sum(first, []) + second:
        copy.start(priority=1)

    down_i = lax.broadcasted_iota(jnp.int32, (toks, toks), 0)
    across = lax.broadcasted_iota(jnp.int32, (toks, toks), 1)

    def column(row):
        spread = jnp.broadcast_to(row.astype(F32), (toks, toks))
        return jnp.sum(jnp.where(across == down_i, spread, 0.0), axis=1, keepdims=True)

    lane = lax.broadcasted_iota(jnp.int32, (toks, seg), 1)
    lane_expert = lax.shift_right_logical(lane, CAP.bit_length() - 1)
    lane_slot = lax.bitwise_and(lane, CAP - 1)
    for copy in small[:3]:
        copy.wait()
    hit0 = column(ids_ref[0:1, :]) == lane_expert.astype(F32)
    hit1 = column(ids_ref[1:2, :]) == lane_expert.astype(F32)
    named = jnp.where(hit0 | hit1, 1.0, 0.0)
    earlier = jnp.where(across < down_i, 1.0, 0.0)
    rank = jnp.dot(earlier.astype(BF16), named.astype(BF16), preferred_element_type=F32)
    placed = jnp.where(rank == lane_slot.astype(F32), named, 0.0)
    placing[...] = placed.astype(BF16)
    member = column(mem_ref[...])
    col = lax.broadcasted_iota(jnp.int32, (toks, LANES), 1)

    def gather(which, data):
        return lax.dot_general(
            which.astype(BF16), data.astype(BF16), (((0,), (0,)), ((), ())), preferred_element_type=F32
        )

    meta_rows = jnp.zeros((seg, LANES), F32)
    for route, hit in ((0, hit0), (1, hit1)):
        meta = jnp.where(col == 0, member, 0.0)
        for spot, piece in enumerate(parts_of(column(cw_ref[route : route + 1, :]))):
            meta = jnp.where(col == 1 + spot, piece, meta)
        meta_rows = meta_rows + gather(jnp.where(hit, placed, 0.0), meta)
    send[:, width:] = meta_rows.astype(BF16)
    small[3].wait()
    for t in range(width // wide):
        cols = slice(t * wide, (t + 1) * wide)
        send[:, cols] = gather(placed, tok_ref[:, cols]).astype(BF16)

    pl.semaphore_wait(barrier, EXPERTS - 1 + split - 1)

    def landed(k, j):
        batch, slot = PLACE[k]
        each = len(BATCHES[batch])
        return rows(batch * split * each + part_at(-j) * each + slot)

    def direct(k):
        return pltpu.make_async_remote_copy(
            src_ref=send.at[rows(expert_at(k))],
            dst_ref=recv.at[landed(k, 0)],
            send_sem=dsend.at[k],
            recv_sem=drecv.at[k],
            device_id=far(k),
            device_id_type=pl.DeviceIdType.MESH,
        )

    def handed(k, j):
        return pltpu.make_async_remote_copy(
            src_ref=recv.at[landed(k, 0)] if k else send.at[rows(own)],
            dst_ref=recv.at[landed(k, 0)],
            send_sem=xsend.at[k, j],
            recv_sem=xrecv.at[k, j],
            device_id=near(j),
            device_id_type=pl.DeviceIdType.MESH,
        )

    for k in SEND_ORDER:
        direct(k).start()
    for j in range(1, split):
        handed(0, j).start()
    recv[landed(0, 0), :] = send[rows(own), :]

    for copy in loads:
        copy.wait()
    for g in range(2):
        for t in range(unit_tiles):
            cols = slice(t * tile, (t + 1) * tile)
            tab_hid[g, :, cols] = hidf_ref[:, g, cols]

    def hand_on(k):
        pltpu.make_async_remote_copy(
            src_ref=recv.at[landed(k, 0)],
            dst_ref=recv.at[landed(k, 0)],
            send_sem=dsend.at[k],
            recv_sem=drecv.at[k],
            device_id=far(k),
            device_id_type=pl.DeviceIdType.MESH,
        ).wait_recv()
        for j in range(1, split):
            handed(k, j).start()

    def got(k, j):
        pltpu.make_async_remote_copy(
            src_ref=recv.at[landed(k, j)],
            dst_ref=recv.at[landed(k, j)],
            send_sem=xsend.at[k, j],
            recv_sem=xrecv.at[k, j],
            device_id=near(j),
            device_id_type=pl.DeviceIdType.MESH,
        ).wait_recv()

    def scale_unit(k, j):
        mine = landed(k, j)
        meta = recv[mine, width:].astype(F32)
        which = jnp.broadcast_to(meta[:, 0:1], (CAP, LANES)).astype(jnp.int32)
        who[mine, :] = which
        if j == 0:
            batch, slot = PLACE[k]
            spot = lax.broadcasted_iota(jnp.int32, (CAP, LANES), 1)
            weight = jnp.sum(
                jnp.where((spot >= 1) & (spot < 4), meta, 0.0), axis=1, keepdims=True
            )
            weigh[batch, slot * CAP : (slot + 1) * CAP, :] = jnp.broadcast_to(weight, (CAP, LANES))
        members = [which[r : r + 8] for r in range(0, CAP, 8)]
        for t in range(width // wide):
            cols = slice(t * wide, (t + 1) * wide)
            data = recv[mine, cols].astype(F32)
            gate_in[mine, cols] = (data * pick(inf[:, cols], members)).astype(BF16)
            cols_up = slice(width + t * wide, width + (t + 1) * wide)
            up_in[mine, cols] = (data * pick(inf[:, cols_up], members)).astype(BF16)

    def hidden_units(b, low, high):
        mine = slice(b * batch_rows, (b + 1) * batch_rows)

        def hidden_tile(t, carry):
            cols = pl.ds(pl.multiple_of(t * tile, tile), tile)
            members = [
                who[b * batch_rows + r : b * batch_rows + r + 8, :] for r in range(0, batch_rows, 8)
            ]
            gate = jnp.dot(gate_in[mine, :], wg[:, cols], preferred_element_type=F32)
            gate = gate * pick(tab_hid[0, :, cols], members)
            up = jnp.dot(up_in[mine, :], wu[:, cols], preferred_element_type=F32)
            up = up * pick(tab_hid[1, :, cols], members)
            hidden[:, cols] = (gate / (1.0 + jnp.exp(-gate)) * up).astype(BF16)
            return carry

        lax.fori_loop(low, high, hidden_tile, 0, unroll=high - low)

    def share(b, t, j):
        return pltpu.make_async_remote_copy(
            src_ref=psend.at[b, t, rows(part_at(j), share_rows)],
            dst_ref=precv.at[b, t, j],
            send_sem=psems.at[b, t, j],
            recv_sem=precs.at[b, t, j],
            device_id=near(j),
            device_id_type=pl.DeviceIdType.MESH,
        )

    def back(t, k):
        batch, slot = PLACE[k]
        return pltpu.make_async_remote_copy(
            src_ref=osend.at[batch, t, pl.ds(slot * CAP, CAP)],
            dst_ref=home.at[t, rows(own)],
            send_sem=hsend.at[t, k],
            recv_sem=hrecv.at[t, k],
            device_id=far(k),
            device_id_type=pl.DeviceIdType.MESH,
        )

    def down_tile(b, t):
        cols = slice(t * out_tile, (t + 1) * out_tile)
        psend[b, t] = jnp.dot(hidden[...], wd[:, cols], preferred_element_type=F32).astype(BF16)
        for j in range(1, split):
            share(b, t, j).start()

    def finish(b, t):
        base = b * batch_rows + part * share_rows
        members = [
            who[pl.ds(pl.multiple_of(base + r, 8), 8), :] for r in range(0, share_rows, 8)
        ]
        total = psend[b, t, rows(part, share_rows), :].astype(F32)
        for j in range(1, split):
            share(b, t, j).wait_recv()
            total = total + precv[b, t, j].astype(F32)
        cols = slice(t * out_tile, (t + 1) * out_tile)
        weight = jnp.concatenate([weigh[b]] * (out_tile // LANES), axis=1)
        value = (total * pick(outf[:, cols], members) * weight).astype(BF16)
        osend[b, t] = value
        for slot, k in enumerate(BATCHES[b]):
            if k:
                back(t, k).start()
            else:
                home[t, rows(own), :] = value[slot * CAP : (slot + 1) * CAP]

    half = (unit_tiles + 1) // 2
    ahead = max(0, tiles - 2)

    scale_unit(0, 0)
    for k in BATCHES[0][1:]:
        hand_on(k)
        scale_unit(k, 0)
    for k in BATCHES[0]:
        for j in range(1, split):
            got(k, j)
            scale_unit(k, j)
    for copies in first[:half]:
        for copy in copies:
            copy.wait()
    hidden_units(0, 0, half)
    for copies in first[half:]:
        for copy in copies:
            copy.wait()
    for k in BATCHES[1][:2]:
        hand_on(k)
    hidden_units(0, half, unit_tiles)
    hand_on(BATCHES[1][2])
    for t in range(tiles):
        second[t].wait()
        down_tile(0, t)
        if t >= 2:
            finish(0, t - 2)
    hand_on(BATCHES[1][3])
    for k in BATCHES[1]:
        scale_unit(k, 0)
    for t in range(ahead, tiles):
        finish(0, t)
    for k in BATCHES[1]:
        for j in range(1, split):
            got(k, j)
            scale_unit(k, j)
    hidden_units(1, 0, unit_tiles)
    for t in range(tiles):
        down_tile(1, t)
        if t >= 2:
            finish(1, t - 2)
    for t in range(ahead, tiles):
        finish(1, t)

    for t in range(tiles):
        cols = slice(t * out_tile, (t + 1) * out_tile)
        for k in range(1, EXPERTS):
            back(t, k).wait_recv()
        o_ref[:, cols] = jnp.dot(placing[...], home[t], preferred_element_type=F32).astype(BF16)

    for k in range(1, EXPERTS):
        direct(k).wait_send()
    for k in range(EXPERTS):
        for j in range(1, split):
            handed(k, j).wait_send()
    for t in range(tiles):
        for b in range(len(BATCHES)):
            for j in range(1, split):
                share(b, t, j).wait_send()
        for k in range(1, EXPERTS):
            back(t, k).wait_send()


def per_device(
    tokens,
    expert_ids,
    member_ids,
    combine_weights,
    gate_weight,
    up_weight,
    down_weight,
    input_factors,
    hidden_factors,
    output_factors,
):
    n = lax.axis_size("expert")
    split = n // EXPERTS
    toks, width = tokens.shape
    units = gate_weight.shape[1]
    members = input_factors.shape[1]
    seg = EXPERTS * CAP
    all_rows = n * CAP
    batches = len(BATCHES)
    batch_rows = all_rows // batches
    out_tile = tile_of(width)
    tiles = width // out_tile
    unit_tiles = units // tile_of(units)
    vmem = pl.BlockSpec(memory_space=pltpu.VMEM)
    hbm = pl.BlockSpec(memory_space=pl.ANY)
    dma = pltpu.SemaphoreType.DMA
    return pl.pallas_call(
        functools.partial(kernel, n),
        out_shape=pltpu.VMEM((toks, width), BF16),
        in_specs=[hbm] * 10,
        out_specs=vmem,
        scratch_shapes=[
            pltpu.VMEM((2, toks), jnp.int32),
            pltpu.VMEM((1, toks), jnp.int32),
            pltpu.VMEM((2, toks), F32),
            pltpu.VMEM((toks, width), BF16),
            pltpu.VMEM(hidden_factors.shape, F32),
            pltpu.VMEM((width, units), BF16),
            pltpu.VMEM((width, units), BF16),
            pltpu.VMEM((units, width), BF16),
            pltpu.VMEM((members, 2 * width), F32),
            pltpu.VMEM((members, width), F32),
            pltpu.VMEM((2, members, units), F32),
            pltpu.VMEM((seg, width + LANES), BF16),
            pltpu.VMEM((all_rows, width + LANES), BF16),
            pltpu.VMEM((all_rows, LANES), jnp.int32),
            pltpu.VMEM((batches, seg // batches, LANES), F32),
            pltpu.VMEM((all_rows, width), BF16),
            pltpu.VMEM((all_rows, width), BF16),
            pltpu.VMEM((batch_rows, units), BF16),
            pltpu.VMEM((batches, tiles, batch_rows, out_tile), BF16),
            pltpu.VMEM((batches, tiles, split, seg // batches, out_tile), BF16),
            pltpu.VMEM((batches, tiles, seg // batches, out_tile), BF16),
            pltpu.VMEM((tiles, seg, out_tile), BF16),
            pltpu.VMEM((toks, seg), BF16),
            dma((3, max(unit_tiles, tiles))),
            dma((7,)),
            dma((EXPERTS,)),
            dma((EXPERTS,)),
            dma((batches, tiles, split)),
            dma((batches, tiles, split)),
            dma((tiles, EXPERTS)),
            dma((tiles, EXPERTS)),
            dma((EXPERTS, split)),
            dma((EXPERTS, split)),
        ],
        compiler_params=pltpu.CompilerParams(
            collective_id=0, has_side_effects=True, vmem_limit_bytes=VMEM_LIMIT
        ),
        name="moe_step",
    )(
        expert_ids.T,
        member_ids.reshape(1, toks),
        combine_weights.T,
        tokens,
        hidden_factors,
        gate_weight,
        up_weight,
        down_weight,
        input_factors,
        output_factors,
    )


def solution(mesh):
    in_specs = (
        P(("groups", "expert"), None),
        P(("groups", "expert"), None),
        P(("groups", "expert")),
        P(("groups", "expert"), None),
        P(None, "expert"),
        P(None, "expert"),
        P("expert", None),
        P(),
        P(None, None, "expert"),
        P(),
    )
    out_specs = P(("groups", "expert"), None)
    return jax.shard_map(
        per_device, mesh=mesh, in_specs=in_specs, out_specs=out_specs, check_vma=False
    )
```

time: 48.7 us -> 41 us (0.84)
  Pallas kernels: 47 us -> 40.2 us
  local copies, waits for them, and re-layouts: 1.57 us -> 0.66 us
    pallas_call x1, Pallas kernels: 47 us -> 40.2 us  [per_device(): pl.pallas_call(functools.partial(kernel, n), out_shape=pltpu.VMEM((toks,...]
    unnamed x1, local copies, waits for them, and re-layouts: 1.57 us -> 0.66 us
where the time goes in v1:
time: 41 us; the launch traced here: 40.9 us
  Pallas kernels  40.2 us (98%)
  local copies, waits for them, and re-layouts  0.66 us (2%)
    pallas_call x1, Pallas kernels, per_device(): pl.pallas_call(functools.partial(kernel, n), out_shape=pltpu.VMEM((toks,...  40.2 us

profile of v1, /device:TPU:0, one launch (start us, length us, event | category | flops | bytes accessed | tf_op | source)
XLA Modules:
  0.0 40.9 jit_solution(13778378423527751329)
XLA Ops:
  0.0 40.2 %moe_step.1 = bf16[32,2048]{1,0:T(8,128)(2,1)S(1)} custom-call(s32[2,32]{1,0:T(2,128)} %bitcast.3, s32[1,32]{1,0:T(1,128)} %bitcast.5, f32[2,32]{1,0:T(2,128)} %bitcast.4, bf16[32,2048]{1,0:T(8,128)(2,1)} %tok_hbm.1, f32[8,2,3584]{2,1,0:T(2,128)} %hidf_hbm.1, bf16[2048,3584]{1,0:T(8,128)(2,1)} %wg_hbm.1, bf16[2048,3584]{1,0:T(8,128)(2,1)} %wu_hbm.1, ...), custom_call_target="tpu_custom_call" | custom-call | tf_op jit(solution)/shard_map/moe_step/pallas_call | solution.py:430
  40.2 0.7 %copy.12 = bf16[32,2048]{1,0:T(8,128)(2,1)} copy(bf16[32,2048]{1,0:T(8,128)(2,1)S(1)} %moe_step.1) | data formatting | bytes 262144

commit v2 on v1

--- a/solution.py
+++ b/solution.py
@@ -12,7 +12,11 @@
 LANES = 128
 VMEM_LIMIT = 63 * 1024 * 1024
 BATCHES = ((0, 1, 4, 6), (2, 3, 5, 7))
-SEND_ORDER = (4, 6, 1, 2, 3, 5, 7)
+LAG = 2
+SEND_ORDER = (4, 6, 1, 2, 3)
+LATER = (5, 7)
+GROUPS = (2, 4)
+RETURNS = ((1, 4, 6), (2, 3, 5, 7))
 PLACE = {k: (b, i) for b, ks in enumerate(BATCHES) for i, k in enumerate(ks)}
 BF16 = jnp.bfloat16
 F32 = jnp.float32
@@ -99,7 +103,9 @@
     wide = tile_of(width)
     tile = tile_of(units)
     unit_tiles = units // tile
-    tiles, _, out_tile = home.shape
+    out_tile = tile_of(width)
+    tiles = width // out_tile
+    ends = [[tiles * (g + 1) // n_g for g in range(n_g)] for n_g in GROUPS]
     batch_rows = recv.shape[0] // len(BATCHES)
     share_rows = batch_rows // split
 
@@ -301,13 +307,15 @@
             device_id_type=pl.DeviceIdType.MESH,
         )
 
-    def back(t, k):
+    def back(g, k):
         batch, slot = PLACE[k]
+        low = ends[batch][g - 1] if g else 0
+        cols = pl.ds(low * out_tile, (ends[batch][g] - low) * out_tile)
         return pltpu.make_async_remote_copy(
-            src_ref=osend.at[batch, t, pl.ds(slot * CAP, CAP)],
-            dst_ref=home.at[t, rows(own)],
-            send_sem=hsend.at[t, k],
-            recv_sem=hrecv.at[t, k],
+            src_ref=osend.at[batch, pl.ds(slot * CAP, CAP), cols],
+            dst_ref=home.at[rows(own), cols],
+            send_sem=hsend.at[g, k],
+            recv_sem=hrecv.at[g, k],
             device_id=far(k),
             device_id_type=pl.DeviceIdType.MESH,
         )
@@ -330,20 +338,23 @@
         cols = slice(t * out_tile, (t + 1) * out_tile)
         weight = jnp.concatenate([weigh[b]] * (out_tile // LANES), axis=1)
         value = (total * pick(outf[:, cols], members) * weight).astype(BF16)
-        osend[b, t] = value
-        for slot, k in enumerate(BATCHES[b]):
-            if k:
-                back(t, k).start()
-            else:
-                home[t, rows(own), :] = value[slot * CAP : (slot + 1) * CAP]
+        osend[b, :, cols] = value
+        if b == PLACE[0][0]:
+            slot = PLACE[0][1]
+            home[rows(own), cols] = value[slot * CAP : (slot + 1) * CAP]
+        if t + 1 in ends[b]:
+            for k in RETURNS[b]:
+                back(ends[b].index(t + 1), k).start()
 
     half = (unit_tiles + 1) // 2
-    ahead = max(0, tiles - 2)
+    ahead = max(0, tiles - LAG)
 
     scale_unit(0, 0)
     for k in BATCHES[0][1:]:
         hand_on(k)
         scale_unit(k, 0)
+    for k in LATER:
+        direct(k).start()
     for k in BATCHES[0]:
         for j in range(1, split):
             got(k, j)
@@ -358,12 +369,13 @@
     for k in BATCHES[1][:2]:
         hand_on(k)
     hidden_units(0, half, unit_tiles)
-    hand_on(BATCHES[1][2])
     for t in range(tiles):
         second[t].wait()
         down_tile(0, t)
-        if t >= 2:
-            finish(0, t - 2)
+        if t >= LAG:
+            finish(0, t - LAG)
+        if t == min(2, tiles - 1):
+            hand_on(BATCHES[1][2])
     hand_on(BATCHES[1][3])
     for k in BATCHES[1]:
         scale_unit(k, 0)
@@ -376,16 +388,21 @@
     hidden_units(1, 0, unit_tiles)
     for t in range(tiles):
         down_tile(1, t)
-        if t >= 2:
-            finish(1, t - 2)
+        if t >= LAG:
+            finish(1, t - LAG)
     for t in range(ahead, tiles):
         finish(1, t)
 
     for t in range(tiles):
         cols = slice(t * out_tile, (t + 1) * out_tile)
         for k in range(1, EXPERTS):
-            back(t, k).wait_recv()
-        o_ref[:, cols] = jnp.dot(placing[...], home[t], preferred_element_type=F32).astype(BF16)
+            stops = ends[PLACE[k][0]]
+            for g, begin in enumerate([0] + stops[:-1]):
+                if begin == t:
+                    back(g, k).wait_recv()
+        o_ref[:, cols] = jnp.dot(
+            placing[...], home[:, cols], preferred_element_type=F32
+        ).astype(BF16)
 
     for k in range(1, EXPERTS):
         direct(k).wait_send()
@@ -396,8 +413,9 @@
         for b in range(len(BATCHES)):
             for j in range(1, split):
                 share(b, t, j).wait_send()
-        for k in range(1, EXPERTS):
-            back(t, k).wait_send()
+    for k in range(1, EXPERTS):
+        for g in range(len(ends[PLACE[k][0]])):
+            back(g, k).wait_send()
 
 
 def per_device(
@@ -453,8 +471,8 @@
             pltpu.VMEM((batch_rows, units), BF16),
             pltpu.VMEM((batches, tiles, batch_rows, out_tile), BF16),
             pltpu.VMEM((batches, tiles, split, seg // batches, out_tile), BF16),
-            pltpu.VMEM((batches, tiles, seg // batches, out_tile), BF16),
-            pltpu.VMEM((tiles, seg, out_tile), BF16),
+            pltpu.VMEM((batches, seg // batches, width), BF16),
+            pltpu.VMEM((seg, width), BF16),
             pltpu.VMEM((toks, seg), BF16),
             dma((3, max(unit_tiles, tiles))),
             dma((7,)),

time: 41 us -> 39.1 us (0.954)
  Pallas kernels: 40.2 us -> 38.3 us
    pallas_call x1, Pallas kernels: 40.2 us -> 38.3 us  [per_device(): pl.pallas_call(functools.partial(kernel, n), out_shape=pltpu.VMEM((toks,...]
where the time goes in v2:
time: 39.1 us; the launch traced here: 39 us
  Pallas kernels  38.3 us (98%)
  local copies, waits for them, and re-layouts  0.66 us (2%)
    pallas_call x1, Pallas kernels, per_device(): pl.pallas_call(functools.partial(kernel, n), out_shape=pltpu.VMEM((toks,...  38.3 us

profile of v2, /device:TPU:0, one launch (start us, length us, event | category | flops | bytes accessed | tf_op | source)
XLA Modules:
  0.0 39.0 jit_solution(16890069951687493325)
XLA Ops:
  0.0 38.3 %moe_step.1 = bf16[32,2048]{1,0:T(8,128)(2,1)S(1)} custom-call(s32[2,32]{1,0:T(2,128)} %bitcast.3, s32[1,32]{1,0:T(1,128)} %bitcast.5, f32[2,32]{1,0:T(2,128)} %bitcast.4, bf16[32,2048]{1,0:T(8,128)(2,1)} %tok_hbm.1, f32[8,2,3584]{2,1,0:T(2,128)} %hidf_hbm.1, bf16[2048,3584]{1,0:T(8,128)(2,1)} %wg_hbm.1, bf16[2048,3584]{1,0:T(8,128)(2,1)} %wu_hbm.1, ...), custom_call_target="tpu_custom_call" | custom-call | tf_op jit(solution)/shard_map/moe_step/pallas_call | solution.py:448
  38.3 0.7 %copy.12 = bf16[32,2048]{1,0:T(8,128)(2,1)} copy(bf16[32,2048]{1,0:T(8,128)(2,1)S(1)} %moe_step.1) | data formatting | bytes 262144

commit v3 on v2

--- a/solution.py
+++ b/solution.py
@@ -13,8 +13,8 @@
 VMEM_LIMIT = 63 * 1024 * 1024
 BATCHES = ((0, 1, 4, 6), (2, 3, 5, 7))
 LAG = 2
-SEND_ORDER = (4, 6, 1, 2, 3)
-LATER = (5, 7)
+SEND_ORDER = (6, 4, 1, 3, 2)
+LATER = (7, 5)
 GROUPS = (2, 4)
 RETURNS = ((1, 4, 6), (2, 3, 5, 7))
 PLACE = {k: (b, i) for b, ks in enumerate(BATCHES) for i, k in enumerate(ks)}

time: 39.1 us -> 40.9 us (1.046)
  Pallas kernels: 38.3 us -> 40.1 us
    pallas_call x1, Pallas kernels: 38.3 us -> 40.1 us  [per_device(): pl.pallas_call(functools.partial(kernel, n), out_shape=pltpu.VMEM((toks,...]
where the time goes in v3:
time: 40.9 us; the launch traced here: 40.8 us
  Pallas kernels  40.1 us (98%)
  local copies, waits for them, and re-layouts  0.66 us (2%)
    pallas_call x1, Pallas kernels, per_device(): pl.pallas_call(functools.partial(kernel, n), out_shape=pltpu.VMEM((toks,...  40.1 us

profile of v3, /device:TPU:0, one launch (start us, length us, event | category | flops | bytes accessed | tf_op | source)
XLA Modules:
  0.0 40.8 jit_solution(13706197357845742109)
XLA Ops:
  0.0 40.1 %moe_step.1 = bf16[32,2048]{1,0:T(8,128)(2,1)S(1)} custom-call(s32[2,32]{1,0:T(2,128)} %bitcast.3, s32[1,32]{1,0:T(1,128)} %bitcast.5, f32[2,32]{1,0:T(2,128)} %bitcast.4, bf16[32,2048]{1,0:T(8,128)(2,1)} %tok_hbm.1, f32[8,2,3584]{2,1,0:T(2,128)} %hidf_hbm.1, bf16[2048,3584]{1,0:T(8,128)(2,1)} %wg_hbm.1, bf16[2048,3584]{1,0:T(8,128)(2,1)} %wu_hbm.1, ...), custom_call_target="tpu_custom_call" | custom-call | tf_op jit(solution)/shard_map/moe_step/pallas_call | solution.py:448
  40.1 0.7 %copy.12 = bf16[32,2048]{1,0:T(8,128)(2,1)} copy(bf16[32,2048]{1,0:T(8,128)(2,1)S(1)} %moe_step.1) | data formatting | bytes 262144
